TPU v7x, 32 devices: a whole 2x2x4 slice. The times are simulated.
32 devices in a mesh: seq: 8 (over z, y), grp: 4 (over x, core).
Axes of the slice: x: 2, y: 2, z: 4, core: 2. Of those that a mesh axis runs over, the one named last changes fastest.
Arguments:
- hidden: bfloat16 [4096, 2048], P('seq', 'grp'), may hold values from -8 to 8
- qkv_weight: bfloat16 [3, 2048, 6144], P(None, 'seq', 'grp'), may hold values from -0.125 to 0.125
- out_weight: bfloat16 [3, 2048, 2048], P(None, 'grp', 'seq'), may hold values from -0.125 to 0.125
- projection: float32 [3, 16, 128, 128], P(None, 'grp'), may hold values from -6 to 6
- norm_gain: float32 [3, 2048], replicated, may hold values from 0.1 to 1.9
- out_gain: float32 [3, 2048], P(None, 'grp'), may hold values from 0.1 to 1.9
Outputs:
- layer_out: bfloat16 [4096, 2048], P('seq', 'grp')
All inputs are finite; a program needn't handle non-finite values.
Results may differ from a plain program's by a relative error of at most 0.034.
Values may be sent and summed in bfloat16 or wider, within the bound.
A program may use at most 64 MiB of HBM per device.

v0:
```python
import math

import jax
import jax.numpy as jnp
from jax import lax
from jax.sharding import PartitionSpec as P

stabilizer = 2.0
highest = lax.Precision.HIGHEST


def prefix(array, axis, combine, identity):
    peers, index = (lax.axis_size(axis), lax.axis_index(axis))
    everything = jax.tree.map(
        lambda part, kind: lax.all_gather(part.astype(kind), axis),
        array,
        (jnp.bfloat16, jnp.bfloat16),
    )
    start = jax.tree.map(
        lambda part, zero: jnp.broadcast_to(jnp.asarray(zero, part.dtype), part.shape),
        array,
        identity,
    )

    def step(k, before):
        reached = k < index
        new = combine(
            before, jax.tree.map(lambda part, own: part[k].astype(own.dtype), everything, array)
        )
        return jax.tree.map(lambda a, b: jnp.where(reached, a, b), new, before)

    return lax.fori_loop(0, peers, step, start)


def features(rows, projection_layer):
    head_size = rows.shape[-1]
    feature_count = projection_layer.shape[-1]
    scaled = rows.astype(jnp.float32) * head_size ** (-0.25)
    mixed = jnp.einsum("thd,hdm->thm", scaled, projection_layer, precision=highest)
    energy = 0.5 * jnp.sum(scaled * scaled, axis=-1, keepdims=True)
    return (jnp.exp(mixed - energy - stabilizer) / math.sqrt(feature_count)).astype(jnp.bfloat16)


def add_states(earlier, later):
    return (earlier[0] + later[0], earlier[1] + later[1])


def local(hidden, qkv_weight, out_weight, projection, norm_gain, out_gain):
    layer_count = qkv_weight.shape[0]
    local_heads = projection.shape[1]
    head_size = projection.shape[2]
    feature_count = projection.shape[3]
    token_rows = hidden.shape[0]
    stream = hidden
    causal_mask = jnp.arange(token_rows)[:, None] >= jnp.arange(token_rows)[None, :]
    for layer_index in range(layer_count):
        gathered = lax.all_gather(stream, "grp", axis=1, tiled=True)
        wide = gathered.astype(jnp.float32)
        inverse_rms = lax.rsqrt(jnp.mean(wide * wide, axis=-1, keepdims=True) + 1e-05)
        normed = (wide * inverse_rms * norm_gain[layer_index][None, :]).astype(jnp.bfloat16)
        qkv_wide = jnp.dot(
            normed,
            lax.all_gather(qkv_weight[layer_index], "seq", axis=0, tiled=True),
            preferred_element_type=jnp.float32,
        )
        qkv = qkv_wide.astype(jnp.bfloat16).reshape(token_rows, local_heads, 3, head_size)
        query_feat = features(qkv[:, :, 0], projection[layer_index])
        key_feat = features(qkv[:, :, 1], projection[layer_index])
        value_rows = qkv[:, :, 2]
        block_kv = jnp.einsum(
            "jhm,jhe->hme", key_feat, value_rows, preferred_element_type=jnp.float32
        )
        block_z = jnp.sum(key_feat.astype(jnp.float32), axis=0)
        zero_kv = jnp.zeros((local_heads, feature_count, head_size), jnp.float32)
        zero_z = jnp.zeros((local_heads, feature_count), jnp.float32)
        prefix_kv, prefix_z = prefix((block_kv, block_z), "seq", add_states, (zero_kv, zero_z))
        scores = jnp.einsum(
            "ihm,jhm->hij", query_feat, key_feat, preferred_element_type=jnp.float32
        )
        masked = jnp.where(causal_mask[None], scores, jnp.zeros_like(scores))
        score_weights = masked.astype(jnp.bfloat16)
        query_wide = query_feat.astype(jnp.float32)
        denominator = jnp.sum(masked, axis=-1) + jnp.einsum(
            "ihm,hm->hi", query_wide, prefix_z, precision=highest
        )
        numerator = jnp.einsum(
            "hij,jhe->hie", score_weights, value_rows, preferred_element_type=jnp.float32
        )
        numerator = numerator + jnp.einsum(
            "ihm,hme->hie",
            query_feat,
            prefix_kv.astype(jnp.bfloat16),
            preferred_element_type=jnp.float32,
        )
        attention = numerator / denominator[..., None]
        inverse_norm = lax.rsqrt(jnp.mean(attention * attention, axis=-1, keepdims=True) + 1e-06)
        head_gain = out_gain[layer_index].reshape(local_heads, head_size)[:, None, :]
        attended = (attention * inverse_norm * head_gain).astype(jnp.bfloat16)
        attended = jnp.transpose(attended, (1, 0, 2)).reshape(token_rows, local_heads * head_size)
        terms = jnp.dot(
            attended,
            lax.all_gather(out_weight[layer_index], "seq", axis=1, tiled=True),
            preferred_element_type=jnp.float32,
        )
        summed = lax.psum_scatter(
            terms.astype(jnp.bfloat16), "grp", scatter_dimension=1, tiled=True
        ).astype(jnp.float32)
        stream = (stream.astype(jnp.float32) + summed).astype(jnp.bfloat16)
    return stream


def solution(mesh):
    return jax.shard_map(
        local,
        mesh=mesh,
        in_specs=(
            P("seq", "grp"),
            P(None, "seq", "grp"),
            P(None, "grp", "seq"),
            P(None, "grp", None, None),
            P(),
            P(None, "grp"),
        ),
        out_specs=P("seq", "grp"),
        check_vma=False,
    )
```

profile of v0, /device:TPU:0, one launch (start us, length us, event | category | flops | bytes accessed | tf_op | source)
XLA Modules:
  0.0 804.3 jit_solution(3640511315558074532)
XLA Ops:
  10.6 23.6 %all-gather.28.cloned.1.call-done = bf16[512,2048]{1,0:T(8,128)(2,1)} async-done(((bf16[512,512]{1,0:T(8,128)(2,1)}), bf16[512,2048]{1,0:T(8,128)(2,1)}) %all-gather.28.cloned.1.call-update) | async-done | bytes 2097168 | tf_op jit(solution)/shard_map/all_gather | solution.py:57
  36.4 98.7 %all-gather.34.cloned.1.call-done = bf16[1,2048,1536]{2,1,0:T(8,128)(2,1)} async-done(((bf16[1,256,1536]{2,1,0:T(8,128)(2,1)}), bf16[1,2048,1536]{2,1,0:T(8,128)(2,1)}) %all-gather.34.cloned.1.call-update) | async-done | bytes 6291472 | tf_op jit(solution)/shard_map/all_gather | solution.py:63
  135.1 7.4 fusion.15
  151.3 17.7 %all-gather.12 = bf16[8,4,128]{2,1,0:T(4,128)(2,1)S(1)} all-gather(bf16[1,4,128]{2,1,0:T(4,128)(2,1)S(1)} %bitcast.327), channel_id=4, replica_groups=mesh['seq'=8,'grp'=4] {'seq'}, dimensions={0}, use_global_device_ids=true | all-gather | bytes 9216 | tf_op jit(solution)/shard_map/all_gather | solution.py:15
  174.0 13.0 %all-gather.36.cloned.1.call-done = bf16[32,128,128]{2,1,0:T(8,128)(2,1)} async-done(((bf16[4,128,128]{2,1,0:T(8,128)(2,1)}), bf16[32,128,128]{2,1,0:T(8,128)(2,1)}) %all-gather.36.cloned.1.call-update) | async-done | bytes 1048592 | tf_op jit(solution)/shard_map/all_gather | solution.py:15
  186.9 8.7 %while.48 = (s32[]{:T(128)}, f32[4,128,128]{2,1,0:T(8,128)S(1)}, f32[4,128]{1,0:T(4,128)S(1)}, s32[]{:T(128)}, bf16[8,4,128,128]{3,2,1,0:T(8,128)(2,1)}, /*index...) while((s32[]{:T(128)}, f32[4,128,128]{2,1,0:T(8,128)S(1)}, f32[4,128]{1,0:T(4,128)S(1)}, ...), condition=%wide.region_5.6_spmd.clone, body=%wide.region_4.5_spmd.clone.sunk | while | flops 264196 | bytes 660595 | solution.py:32
  198.1 39.8 %all-gather.38.cloned.1.call-done = bf16[1,512,2048]{2,1,0:T(8,128)(2,1)} async-done(((bf16[1,512,256]{2,1,0:T(8,128)(2,1)}), bf16[1,512,2048]{2,1,0:T(8,128)(2,1)}) %all-gather.38.cloned.1.call-update) | async-done | bytes 2097168 | tf_op jit(solution)/shard_map/all_gather | solution.py:102
  242.2 29.4 %reduce-scatter.4.cloned.1.call-done = bf16[512,512]{1,0:T(8,128)(2,1)} async-done(((bf16[512,2048]{1,0:T(8,128)(2,1)}), bf16[512,512]{1,0:T(8,128)(2,1)}) %reduce-scatter.4.cloned.1.call-update) | async-done | bytes 524304 | tf_op jit(solution)/shard_map/reduce_scatter | solution.py:105
  274.6 21.8 %all-gather.30.cloned.1.call-done = bf16[512,2048]{1,0:T(8,128)(2,1)} async-done(((bf16[512,512]{1,0:T(8,128)(2,1)}), bf16[512,2048]{1,0:T(8,128)(2,1)}) %all-gather.30.cloned.1.call-update) | async-done | bytes 2097168 | tf_op jit(solution)/shard_map/all_gather | solution.py:57
  298.6 98.7 %all-gather.40.cloned.1.call-done = bf16[1,2048,1536]{2,1,0:T(8,128)(2,1)} async-done(((bf16[1,256,1536]{2,1,0:T(8,128)(2,1)}), bf16[1,2048,1536]{2,1,0:T(8,128)(2,1)}) %all-gather.40.cloned.1.call-update) | async-done | bytes 6291472 | tf_op jit(solution)/shard_map/all_gather | solution.py:63
  397.3 7.4 fusion.18
  411.2 17.7 %all-gather.13 = bf16[8,4,128]{2,1,0:T(4,128)(2,1)S(1)} all-gather(bf16[1,4,128]{2,1,0:T(4,128)(2,1)S(1)} %bitcast.329), channel_id=8, replica_groups=mesh['seq'=8,'grp'=4] {'seq'}, dimensions={0}, use_global_device_ids=true | all-gather | bytes 9216 | tf_op jit(solution)/shard_map/all_gather | solution.py:15
  433.9 15.0 %all-gather.42.cloned.1.call-done = bf16[32,128,128]{2,1,0:T(8,128)(2,1)} async-done(((bf16[4,128,128]{2,1,0:T(8,128)(2,1)}), bf16[32,128,128]{2,1,0:T(8,128)(2,1)}) %all-gather.42.cloned.1.call-update) | async-done | bytes 1048592 | tf_op jit(solution)/shard_map/all_gather | solution.py:15
  449.0 8.7 %while.49 = (s32[]{:T(128)}, f32[4,128,128]{2,1,0:T(8,128)S(1)}, f32[4,128]{1,0:T(4,128)S(1)}, s32[]{:T(128)}, bf16[8,4,128,128]{3,2,1,0:T(8,128)(2,1)}, /*index...) while((s32[]{:T(128)}, f32[4,128,128]{2,1,0:T(8,128)S(1)}, f32[4,128]{1,0:T(4,128)S(1)}, ...), condition=%wide.region_14.15_spmd.clone, body=%wide.region_13.14_spmd.clone.sunk | while | flops 264196 | bytes 660595 | solution.py:32
  460.1 40.0 %all-gather.44.cloned.1.call-done = bf16[1,512,2048]{2,1,0:T(8,128)(2,1)} async-done(((bf16[1,512,256]{2,1,0:T(8,128)(2,1)}), bf16[1,512,2048]{2,1,0:T(8,128)(2,1)}) %all-gather.44.cloned.1.call-update) | async-done | bytes 2097168 | tf_op jit(solution)/shard_map/all_gather | solution.py:102
  504.4 29.4 %reduce-scatter.6.cloned.1.call-done = bf16[512,512]{1,0:T(8,128)(2,1)} async-done(((bf16[512,2048]{1,0:T(8,128)(2,1)}), bf16[512,512]{1,0:T(8,128)(2,1)}) %reduce-scatter.6.cloned.1.call-update) | async-done | bytes 524304 | tf_op jit(solution)/shard_map/reduce_scatter | solution.py:105
  536.7 21.9 %all-gather.32.cloned.1.call-done = bf16[512,2048]{1,0:T(8,128)(2,1)} async-done(((bf16[512,512]{1,0:T(8,128)(2,1)}), bf16[512,2048]{1,0:T(8,128)(2,1)}) %all-gather.32.cloned.1.call-update) | async-done | bytes 2097168 | tf_op jit(solution)/shard_map/all_gather | solution.py:57
  560.8 98.5 %all-gather.46.cloned.1.call-done = bf16[1,2048,1536]{2,1,0:T(8,128)(2,1)} async-done(((bf16[1,256,1536]{2,1,0:T(8,128)(2,1)}), bf16[1,2048,1536]{2,1,0:T(8,128)(2,1)}) %all-gather.46.cloned.1.call-update) | async-done | bytes 6291472 | tf_op jit(solution)/shard_map/all_gather | solution.py:63
  659.3 7.4 fusion.21
  673.1 17.7 %all-gather.14 = bf16[8,4,128]{2,1,0:T(4,128)(2,1)S(1)} all-gather(bf16[1,4,128]{2,1,0:T(4,128)(2,1)S(1)} %bitcast.328), channel_id=12, replica_groups=mesh['seq'=8,'grp'=4] {'seq'}, dimensions={0}, use_global_device_ids=true | all-gather | bytes 9216 | tf_op jit(solution)/shard_map/all_gather | solution.py:15
  695.8 15.3 %all-gather.48.cloned.1.call-done = bf16[32,128,128]{2,1,0:T(8,128)(2,1)} async-done(((bf16[4,128,128]{2,1,0:T(8,128)(2,1)}), bf16[32,128,128]{2,1,0:T(8,128)(2,1)}) %all-gather.48.cloned.1.call-update) | async-done | bytes 1048592 | tf_op jit(solution)/shard_map/all_gather | solution.py:15
  711.1 8.7 %while.50 = (s32[]{:T(128)}, f32[4,128,128]{2,1,0:T(8,128)S(1)}, f32[4,128]{1,0:T(4,128)S(1)}, s32[]{:T(128)}, bf16[8,4,128,128]{3,2,1,0:T(8,128)(2,1)}, /*index...) while((s32[]{:T(128)}, f32[4,128,128]{2,1,0:T(8,128)S(1)}, f32[4,128]{1,0:T(4,128)S(1)}, ...), condition=%wide.region_23.24_spmd.clone, body=%wide.region_22.23_spmd.clone.sunk | while | flops 264196 | bytes 660595 | solution.py:32
  722.3 39.8 %all-gather.50.cloned.1.call-done = bf16[1,512,2048]{2,1,0:T(8,128)(2,1)} async-done(((bf16[1,512,256]{2,1,0:T(8,128)(2,1)}), bf16[1,512,2048]{2,1,0:T(8,128)(2,1)}) %all-gather.50.cloned.1.call-update) | async-done | bytes 2097168 | tf_op jit(solution)/shard_map/all_gather | solution.py:102
  766.3 29.5 %reduce-scatter.8.cloned.1.call-done = bf16[512,512]{1,0:T(8,128)(2,1)} async-done(((bf16[512,2048]{1,0:T(8,128)(2,1)}), bf16[512,512]{1,0:T(8,128)(2,1)}) %reduce-scatter.8.cloned.1.call-update) | async-done | bytes 524304 | tf_op jit(solution)/shard_map/reduce_scatter | solution.py:105
  (189 shorter events, 100.1 us)
Async XLA Ops:
  6.5 27.7 %all-gather.28.cloned.1.call-start = ((), (), s32[]{:S(2)}) async-start(), calls=%async_computation.3 | async-start | bytes 2621440 | tf_op jit(solution)/shard_map/all_gather | solution.py:57
  7.3 127.9 %all-gather.34.cloned.1.call-start = ((), (), s32[]{:S(2)}) async-start(), calls=%async_computation.9 | async-start | bytes 7077888 | tf_op jit(solution)/shard_map/all_gather | solution.py:63
  10.5 176.4 %all-gather.36.cloned.1.call-start = ((), (), s32[]{:S(2)}) async-start(), calls=%async_computation.10 | async-start | bytes 1179648 | tf_op jit(solution)/shard_map/all_gather | solution.py:15
  34.2 100.9 %copy-start.3 = (bf16[512,2048]{1,0:T(8,128)(2,1)S(1)}, bf16[512,2048]{1,0:T(8,128)(2,1)}, u32[]{:S(2)}) copy-start(bf16[512,2048]{1,0:T(8,128)(2,1)} %all-gather.28.cloned.1.call-done) | copy-start | bytes 6291460
  148.3 89.6 %all-gather.38.cloned.1.call-start = ((), (), s32[]{:S(2)}) async-start(), calls=%async_computation.11 | async-start | bytes 2359296 | tf_op jit(solution)/shard_map/all_gather | solution.py:102
  150.4 121.2 %reduce-scatter.4.cloned.1.call-start = ((), (), s32[]{:S(2)}) async-start(), calls=%async_computation.4 | async-start | bytes 2621440 | tf_op jit(solution)/shard_map/reduce_scatter | solution.py:105
  186.9 9.6 %copy-start.7 = (pred[512,512]{0,1:T(8,128)(4,1)S(1)}, pred[512,512]{0,1:T(8,128)(4,1)}, u32[]{:S(2)}) copy-start(pred[512,512]{0,1:T(8,128)(4,1)} %iota_compare_fusion) | copy-start | bytes 786436
  242.1 29.5 %copy-start.2 = (bf16[512,512]{1,0:T(8,128)(2,1)S(1)}, bf16[512,512]{1,0:T(8,128)(2,1)}, u32[]{:S(2)}) copy-start(bf16[512,512]{1,0:T(8,128)(2,1)} %param.12) | copy-start | bytes 1572868
  242.1 54.2 %all-gather.30.cloned.1.call-start = ((), (), s32[]{:S(2)}) async-start(), calls=%async_computation.5 | async-start | bytes 2621440 | tf_op jit(solution)/shard_map/all_gather | solution.py:57
  273.6 123.6 %all-gather.40.cloned.1.call-start = ((), (), s32[]{:S(2)}) async-start(), calls=%async_computation.12 | async-start | bytes 7077888 | tf_op jit(solution)/shard_map/all_gather | solution.py:63
  274.4 174.6 %all-gather.42.cloned.1.call-start = ((), (), s32[]{:S(2)}) async-start(), calls=%async_computation.13 | async-start | bytes 1179648 | tf_op jit(solution)/shard_map/all_gather | solution.py:15
  296.3 100.9 %copy-start.5 = (bf16[512,2048]{1,0:T(8,128)(2,1)S(1)}, bf16[512,2048]{1,0:T(8,128)(2,1)}, u32[]{:S(2)}) copy-start(bf16[512,2048]{1,0:T(8,128)(2,1)} %all-gather.30.cloned.1.call-done) | copy-start | bytes 6291460
  410.4 89.7 %all-gather.44.cloned.1.call-start = ((), (), s32[]{:S(2)}) async-start(), calls=%async_computation.14 | async-start | bytes 2359296 | tf_op jit(solution)/shard_map/all_gather | solution.py:102
  411.2 122.7 %reduce-scatter.6.cloned.1.call-start = ((), (), s32[]{:S(2)}) async-start(), calls=%async_computation.6 | async-start | bytes 2621440 | tf_op jit(solution)/shard_map/reduce_scatter | solution.py:105
  449.0 9.6 %copy-start.9 = (pred[512,512]{0,1:T(8,128)(4,1)S(1)}, pred[512,512]{0,1:T(8,128)(4,1)}, u32[]{:S(2)}) copy-start(pred[512,512]{0,1:T(8,128)(4,1)} %iota_compare_fusion) | copy-start | bytes 786436
  504.3 29.5 %copy-start.1 = (bf16[512,512]{1,0:T(8,128)(2,1)S(1)}, bf16[512,512]{1,0:T(8,128)(2,1)}, u32[]{:S(2)}) copy-start(bf16[512,512]{1,0:T(8,128)(2,1)} %add_convert_fusion.2) | copy-start | bytes 1572868
  504.3 54.2 %all-gather.32.cloned.1.call-start = ((), (), s32[]{:S(2)}) async-start(), calls=%async_computation.7 | async-start | bytes 2621440 | tf_op jit(solution)/shard_map/all_gather | solution.py:57
  535.8 123.5 %all-gather.46.cloned.1.call-start = ((), (), s32[]{:S(2)}) async-start(), calls=%async_computation.15 | async-start | bytes 7077888 | tf_op jit(solution)/shard_map/all_gather | solution.py:63
  536.4 174.7 %all-gather.48.cloned.1.call-start = ((), (), s32[]{:S(2)}) async-start(), calls=%async_computation.16 | async-start | bytes 1179648 | tf_op jit(solution)/shard_map/all_gather | solution.py:15
  558.5 100.8 %copy-start.4 = (bf16[512,2048]{1,0:T(8,128)(2,1)S(1)}, bf16[512,2048]{1,0:T(8,128)(2,1)}, u32[]{:S(2)}) copy-start(bf16[512,2048]{1,0:T(8,128)(2,1)} %all-gather.32.cloned.1.call-done) | copy-start | bytes 6291460
  672.5 89.6 %all-gather.50.cloned.1.call-start = ((), (), s32[]{:S(2)}) async-start(), calls=%async_computation.17 | async-start | bytes 2359296 | tf_op jit(solution)/shard_map/all_gather | solution.py:102
  673.1 122.7 %reduce-scatter.8.cloned.1.call-start = ((), (), s32[]{:S(2)}) async-start(), calls=%async_computation.8 | async-start | bytes 2621440 | tf_op jit(solution)/shard_map/reduce_scatter | solution.py:105
  711.1 9.6 %copy-start.11 = (pred[512,512]{0,1:T(8,128)(4,1)S(1)}, pred[512,512]{0,1:T(8,128)(4,1)}, u32[]{:S(2)}) copy-start(pred[512,512]{0,1:T(8,128)(4,1)} %iota_compare_fusion) | copy-start | bytes 786436
  766.3 29.5 %copy-start = (bf16[512,512]{1,0:T(8,128)(2,1)S(1)}, bf16[512,512]{1,0:T(8,128)(2,1)}, u32[]{:S(2)}) copy-start(bf16[512,512]{1,0:T(8,128)(2,1)} %add_convert_fusion.1) | copy-start | bytes 1572868
  (8 other events, 20.0 us)
Sparse Core Ops, SparseCore 0:
  8.9 25.2 all-gather.27
  36.4 98.6 all-gather.33
  148.4 38.4 all-gather.35
  188.8 49.0 all-gather.37
  242.2 29.3 reduce-scatter.3
  273.7 22.5 all-gather.29
  298.5 98.6 all-gather.39
  410.5 38.3 all-gather.41
  451.0 49.0 all-gather.43
  504.5 29.3 reduce-scatter.5
  535.9 22.5 all-gather.31
  560.6 98.6 all-gather.45
  672.6 38.4 all-gather.47
  713.0 49.0 all-gather.49
  766.4 29.3 reduce-scatter.7
where the time goes:
time: 806 us; the launch traced here: 804 us
  waiting for transfers between devices  618 us (77%)
  matrix products  62 us (8%)
  blocking collectives  53.2 us (7%)
  other arithmetic  41.7 us (5%)
  local copies, waits for them, and re-layouts  14.5 us (2%)
  between operations  13.8 us (2%)
    all_gather x3, waiting for transfers between devices, local(): lax.all_gather(qkv_weight[layer_index], 'seq', axis=0, tiled=True)  296 us
    all_gather x3, waiting for transfers between devices, local(): lax.all_gather(out_weight[layer_index], 'seq', axis=1, tiled=True)  120 us
    reduce_scatter x3, waiting for transfers between devices, local(): lax.psum_scatter(terms.astype(jnp.bfloat16), 'grp', scatter_dimension=1,...  88.4 us
    all_gather x3, waiting for transfers between devices, local(): gathered = lax.all_gather(stream, 'grp', axis=1, tiled=True)  67.3 us
    all_gather x3, blocking collectives, prefix(): lax.all_gather(part.astype(kind), axis)  53.2 us
    all_gather x3, waiting for transfers between devices, prefix(): lax.all_gather(part.astype(kind), axis)  43.3 us
    select_n x48, other arithmetic, step(): return jax.tree.map(lambda a, b: jnp.where(reached, a, b), new, before)  25.5 us
    dot_general x3, matrix products, local(): jnp.dot(normed, lax.all_gather(qkv_weight[layer_index], 'seq', axis=0, ti...  22.3 us
  transfers between devices with their start and end apart: 15, of which 15 were waited for; matrix products, arithmetic and copies ran while one was open for 7% of the time, Pallas kernels for 0%

commit v1 on v0

v1 whole, which is shorter than its diff:
```python
import functools
import math

import jax
import jax.numpy as jnp
from jax import lax
from jax.experimental import pallas as pl
from jax.experimental.pallas import tpu as pltpu
from jax.sharding import PartitionSpec as P

MESH = pl.DeviceIdType.MESH
stabilizer = 2.0
f32 = jnp.float32
bf16 = jnp.bfloat16


def remote(src, dst, send, recv, device):
    return pltpu.make_async_remote_copy(
        src_ref=src, dst_ref=dst, send_sem=send, recv_sem=recv, device_id=device, device_id_type=MESH
    )


def kernel(
    n_seq, n_grp, hidden, qkv_w, out_w, proj, norm_gain, out_gain, out,
    wq, wo, xg, part, rs, normed, qf, kf, vf, num, den, att,
    own_state, st_send, st_pair, ps_send, st_line, prefix,
    local_sem, z_send, z_recv, y_send, y_recv, p_send, p_recv, l_send, l_recv,
    ag_send, ag_recv, rs_send, rs_recv,
):
    layers, rows, cols = qkv_w.shape
    oc = out_w.shape[2]
    tokens, width = hidden.shape
    heads = proj.shape[1]
    head = proj.shape[2]
    feats = proj.shape[3] // 3
    lines = n_seq // 2
    me = lax.axis_index("seq")
    grp = lax.axis_index("grp")
    line, parity = me // 2, me % 2
    pair = line * 2 + 1 - parity

    stores = ((qkv_w, wq), (out_w, wo))
    own_copies = [
        [pltpu.make_async_copy(src.at[l], dst.at[l, me], local_sem.at[1 + 2 * l + k]) for k, (src, dst) in enumerate(stores)]
        for l in range(layers)
    ]
    own_hidden = pltpu.make_async_copy(hidden, xg.at[grp], local_sem.at[0])
    own_hidden.start()
    for pair_copies in own_copies:
        for c in pair_copies:
            c.start()

    barrier = pltpu.get_barrier_semaphore()
    for k in range(1, lines):
        pl.semaphore_signal(barrier, inc=1, device_id={"seq": lax.rem(line + k, lines) * 2 + parity}, device_id_type=MESH)
    pl.semaphore_signal(barrier, inc=1, device_id={"seq": pair}, device_id_type=MESH)
    for k in range(1, n_grp):
        pl.semaphore_signal(barrier, inc=1, device_id={"grp": lax.rem(grp + k, n_grp)}, device_id_type=MESH)
    pl.semaphore_wait(barrier, lines + n_grp - 1)

    def z_copy(l, k, step):
        ref = stores[k][1].at[l, me]
        to = lax.rem(line + step, lines) * 2 + parity
        return remote(ref, ref, z_send.at[l, k, step], z_recv.at[l, k, line], {"seq": to})

    def z_arrival(l, k, step):
        src = lax.rem(line + lines - step, lines)
        ref = stores[k][1].at[l, src * 2 + parity]
        return remote(ref, ref, z_send.at[l, k, step], z_recv.at[l, k, src], {"seq": src * 2 + parity})

    def y_copy(l, k, step):
        src = lax.rem(line + lines - step, lines)
        ref = stores[k][1].at[l, src * 2 + parity]
        return remote(ref, ref, y_send.at[l, k, src], y_recv.at[l, k, src], {"seq": pair})

    def y_arrival(l, k, step):
        src = lax.rem(line + lines - step, lines)
        ref = stores[k][1].at[l, src * 2 + 1 - parity]
        return remote(ref, ref, y_send.at[l, k, src], y_recv.at[l, k, src], {"seq": pair})

    def send_weights(l, k):
        own_copies[l][k].wait()
        for step in range(1, lines):
            z_copy(l, k, step).start()
        y_copy(l, k, 0).start()

    def forward(l, k, step):
        z_arrival(l, k, step).wait_recv()
        y_copy(l, k, step).start()

    def ag_copy(l, k):
        to = lax.rem(grp + k, n_grp)
        return remote(xg.at[grp], xg.at[grp], ag_send.at[l, k], ag_recv.at[l, grp], {"grp": to})

    def ag_arrival(l, k):
        src = lax.rem(grp + k, n_grp)
        return remote(xg.at[src], xg.at[src], ag_send.at[l, k], ag_recv.at[l, src], {"grp": src})

    def rs_copy(l, k):
        to = lax.rem(grp + k, n_grp)
        return remote(part.at[to], rs.at[grp], rs_send.at[l, k], rs_recv.at[l, grp], {"grp": to})

    def rs_arrival(l, k):
        src = lax.rem(grp + k, n_grp)
        return remote(part.at[src], rs.at[src], rs_send.at[l, k], rs_recv.at[l, src], {"grp": src})

    def pair_copy(l):
        return remote(st_send.at[l], st_pair.at[l], p_send.at[l], p_recv.at[l], {"seq": pair})

    def line_copy(l, step):
        return remote(
            ps_send.at[l], st_line.at[l, line], l_send.at[l, step], l_recv.at[l, line],
            {"seq": lax.rem(line + step, lines) * 2 + parity},
        )

    def line_arrival(l, step):
        src = lax.rem(line + lines - step, lines)
        return remote(ps_send.at[l], st_line.at[l, src], l_send.at[l, step], l_recv.at[l, src], {"seq": src * 2 + parity})

    own_hidden.wait()
    for k in range(1, n_grp):
        ag_copy(0, k).start()
    send_weights(0, 0)
    send_weights(0, 1)

    scale = head ** (-0.25)
    inv = 1.0 / math.sqrt(feats)

    def features(u, terms):
        mixed = jnp.dot(u, terms, preferred_element_type=f32)
        mixed = (mixed[:, 2 * feats :] + mixed[:, feats : 2 * feats]) + mixed[:, :feats]
        w0 = u.astype(f32) * scale
        energy = 0.5 * jnp.sum(w0 * w0, axis=-1, keepdims=True)
        return (jnp.exp(mixed - energy - stabilizer) * inv).astype(bf16)

    forwarded = 0
    for l in range(layers):
        last = l == layers - 1
        for k in range(1, n_grp):
            ag_copy(l, k).wait_send()
            ag_arrival(l, k).wait_recv()

        @pl.loop(0, tokens // 64)
        def _(t):
            at = pl.ds(pl.multiple_of(t * 64, 64), 64)
            wide = [xg[g, at, :].astype(f32) for g in range(n_grp)]
            total = sum(jnp.sum(v * v, axis=-1, keepdims=True) for v in wide)
            rms = lax.rsqrt(total / (width * n_grp) + 1e-05)
            for g in range(n_grp):
                cut = slice(g * width, (g + 1) * width)
                normed[at, cut] = (wide[g] * rms * norm_gain[l : l + 1, cut]).astype(bf16)

        for step in range(1 + forwarded, lines):
            forward(l, 0, step)
        for step in range(lines):
            y_arrival(l, 0, step).wait_recv()

        @pl.loop(0, heads)
        def _(h):
            at = pl.ds(pl.multiple_of(h * 3 * head, 128), 3 * head)
            w = wq[l, :, :, at].reshape(n_seq * rows, 3 * head)
            qkv = jnp.dot(normed[...], w, preferred_element_type=f32).astype(bf16)
            terms = proj[l, h]
            key = features(qkv[:, head : 2 * head], terms)
            value = qkv[:, 2 * head :]
            qf[h] = features(qkv[:, :head], terms)
            kf[h] = key
            vf[h] = value
            kv = lax.dot_general(key, value, (((0,), (0,)), ((), ())), preferred_element_type=f32)
            z = jnp.dot(jnp.ones((16, tokens), bf16), key, preferred_element_type=f32)
            own_state[h, :feats] = kv
            own_state[h, feats:] = z
            st_send[l, h, :feats] = kv.astype(bf16)
            st_send[l, h, feats:] = z.astype(bf16)

        pair_copy(l).start()
        for step in range(1, lines):
            forward(l, 1, step)
        pair_copy(l).wait_recv()

        @pl.loop(0, heads)
        def _(h):
            ps_send[l, h] = (own_state[h] + st_pair[l, h].astype(f32)).astype(bf16)

        for step in range(1, lines):
            @pl.when(line + step < lines)
            def _(step=step):
                line_copy(l, step).start()

        if not last:
            send_weights(l + 1, 0)
            send_weights(l + 1, 1)

        @pl.loop(0, heads)
        def _(h):
            scores = lax.dot_general(qf[h], kf[h], (((1,), (1,)), ((), ())), preferred_element_type=f32)
            r = lax.broadcasted_iota(jnp.int32, (tokens, tokens), 0)
            c = lax.broadcasted_iota(jnp.int32, (tokens, tokens), 1)
            masked = jnp.where(r >= c, scores, 0.0)
            den[h] = jnp.broadcast_to(jnp.sum(masked, axis=-1, keepdims=True), (tokens, head))
            num[h] = jnp.dot(masked.astype(bf16), vf[h], preferred_element_type=f32)

        odd = jnp.where(parity == 1, 1.0, 0.0)

        @pl.loop(0, heads)
        def _(h):
            prefix[h] = st_pair[l, h].astype(f32) * odd

        for step in range(1, lines):
            @pl.when(line >= step)
            def _(step=step):
                line_arrival(l, step).wait_recv()
                src = lax.rem(line + lines - step, lines)

                @pl.loop(0, heads)
                def _(h):
                    prefix[h] = prefix[h] + st_line[l, src, h].astype(f32)

        @pl.loop(0, heads)
        def _(h):
            q = qf[h]
            z = prefix[h, feats : feats + 1]
            d = den[h] + jnp.sum(q.astype(f32) * z, axis=-1, keepdims=True)
            n = num[h] + jnp.dot(q, prefix[h, :feats].astype(bf16), preferred_element_type=f32)
            a = n / d
            norm = lax.rsqrt(jnp.mean(a * a, axis=-1, keepdims=True) + 1e-06)
            att[:, pl.ds(pl.multiple_of(h * head, 128), head)] = (a * norm * out_gain[l, h]).astype(bf16)

        for step in range(lines):
            y_arrival(l, 1, step).wait_recv()
        per = width // oc
        for k in list(range(1, n_grp)) + [0]:
            to = lax.rem(grp + k, n_grp)
            for i in range(per):
                part[to, :, i * oc : (i + 1) * oc] = jnp.dot(
                    att[...], wo[l, to * per + i], preferred_element_type=f32
                ).astype(bf16)
            if k:
                rs_copy(l, k).start()
        forwarded = 0
        if not last and lines > 1:
            forward(l + 1, 0, 1)
            forwarded = 1
        for k in range(1, n_grp):
            rs_copy(l, k).wait_send()
            rs_arrival(l, k).wait_recv()

        @pl.loop(0, tokens // 64)
        def _(t):
            at = pl.ds(pl.multiple_of(t * 64, 64), 64)
            total = part[grp, at, :].astype(f32)
            for k in range(1, n_grp):
                total = total + rs[lax.rem(grp + k, n_grp), at, :].astype(f32)
            total = (xg[grp, at, :].astype(f32) + total).astype(bf16)
            if last:
                out[at, :] = total
            else:
                xg[grp, at, :] = total

        if not last:
            for k in range(1, n_grp):
                ag_copy(l + 1, k).start()
            if lines > 2:
                forward(l + 1, 0, 2)
                forwarded = 2

    for l in range(layers):
        pair_copy(l).wait_send()
        for k in range(2):
            for step in range(1, lines):
                z_copy(l, k, step).wait_send()
            for step in range(lines):
                y_copy(l, k, step).wait_send()
        for step in range(1, lines):
            @pl.when(line + step < lines)
            def _(step=step):
                line_copy(l, step).wait_send()


def local(n_seq, n_grp, hidden, qkv_weight, out_weight, projection, norm_gain, out_gain):
    layers, rows, cols = qkv_weight.shape
    depth, oc = out_weight.shape[1:]
    heads, head, feats = projection.shape[1:]
    tokens, width = hidden.shape
    lines = n_seq // 2
    scaled = projection * head ** (-0.25)
    high = lax.reduce_precision(scaled, 8, 7)
    rest = scaled - high
    mid = lax.reduce_precision(rest, 8, 7)
    low = rest - mid
    terms = jnp.concatenate([high, mid, low], axis=-1).astype(bf16)
    gains = out_gain.reshape(layers, heads, 1, head)
    dma = pltpu.SemaphoreType.DMA
    vmem = pl.BlockSpec(memory_space=pltpu.VMEM)
    anywhere = pl.BlockSpec(memory_space=pl.ANY)
    state = (heads, feats + 16, head)
    return pl.pallas_call(
        functools.partial(kernel, n_seq, n_grp),
        out_shape=jax.ShapeDtypeStruct((tokens, width), bf16),
        in_specs=[anywhere, anywhere, anywhere, vmem, vmem, vmem],
        out_specs=vmem,
        scratch_shapes=[
            pltpu.VMEM((layers, n_seq, rows, cols), bf16),
            pltpu.VMEM((layers, n_seq, depth, oc), bf16),
            pltpu.VMEM((n_grp, tokens, width), bf16),
            pltpu.VMEM((n_grp, tokens, width), bf16),
            pltpu.VMEM((n_grp, tokens, width), bf16),
            pltpu.VMEM((tokens, n_grp * width), bf16),
            pltpu.VMEM((heads, tokens, feats), bf16),
            pltpu.VMEM((heads, tokens, feats), bf16),
            pltpu.VMEM((heads, tokens, head), bf16),
            pltpu.VMEM((heads, tokens, head), f32),
            pltpu.VMEM((heads, tokens, head), f32),
            pltpu.VMEM((tokens, heads * head), bf16),
            pltpu.VMEM(state, f32),
            pltpu.VMEM((layers,) + state, bf16),
            pltpu.VMEM((layers,) + state, bf16),
            pltpu.VMEM((layers,) + state, bf16),
            pltpu.VMEM((layers, lines) + state, bf16),
            pltpu.VMEM(state, f32),
            dma((1 + 2 * layers,)),
            dma((layers, 2, lines)),
            dma((layers, 2, lines)),
            dma((layers, 2, lines)),
            dma((layers, 2, lines)),
            dma((layers,)),
            dma((layers,)),
            dma((layers, lines)),
            dma((layers, lines)),
            dma((layers, n_grp)),
            dma((layers, n_grp)),
            dma((layers, n_grp)),
            dma((layers, n_grp)),
        ],
        compiler_params=pltpu.CompilerParams(
            collective_id=0, has_side_effects=True, vmem_limit_bytes=66_000_000
        ),
    )(hidden, qkv_weight, out_weight, terms, norm_gain, gains)


def solution(mesh):
    return jax.shard_map(
        functools.partial(local, mesh.shape["seq"], mesh.shape["grp"]),
        mesh=mesh,
        in_specs=(
            P("seq", "grp"),
            P(None, "seq", "grp"),
            P(None, "grp", "seq"),
            P(None, "grp", None, None),
            P(),
            P(None, "grp"),
        ),
        out_specs=P("seq", "grp"),
        check_vma=False,
    )
```

time: 806 us -> 393 us (0.49)
  waiting for transfers between devices: 618 us -> 0 us
  Pallas kernels: 0 us -> 384 us
  matrix products: 62 us -> 0 us
  blocking collectives: 53.2 us -> 0 us
  other arithmetic: 41.7 us -> 2.65 us
  between operations: 13.8 us -> 0.02 us
  local copies, waits for them, and re-layouts: 14.5 us -> 2.48 us
    all_gather x12 -> x0, waiting for transfers between devices: 526 us -> none  [the longest x3 296 us: local(): lax.all_gather(qkv_weight[layer_index], 'seq', axis=0, tiled=True)]
    pallas_call x0 -> x1, Pallas kernels: none -> 384 us  [local(): pl.pallas_call(functools.partial(kernel, n_seq, n_grp), out_shape=jax.Sha...]
    reduce_scatter x3 -> x0, waiting for transfers between devices: 88.4 us -> none  [local(): lax.psum_scatter(terms.astype(jnp.bfloat16), 'grp', scatter_dimension=1,...]
    dot_general x27 -> x0, matrix products: 62 us -> none  [the longest x3 22.3 us: local(): jnp.dot(normed, lax.all_gather(qkv_weight[layer_index], 'seq', axis=0, ti...]
    all_gather x3 -> x0, blocking collectives: 53.2 us -> none  [prefix(): lax.all_gather(part.astype(kind), axis)]
    select_n x48 -> x0, other arithmetic: 25.5 us -> none  [step(): return jax.tree.map(lambda a, b: jnp.where(reached, a, b), new, before)]
    reduce_sum x9 -> x0, other arithmetic: 8.8 us -> none  [the longest x3 6.67 us: local(): jnp.mean(wide * wide, axis=-1, keepdims=True) + 1e-05]
  transfers between devices with their start and end apart: 15 -> 0, of which waited for: 15 -> 0; matrix products, arithmetic and copies ran while one was open for 7% -> 0% of each run, Pallas kernels for 0% -> 0%
where the time goes in v1:
time: 393 us; the launch traced here: 389 us
  Pallas kernels  384 us (98%)
    pallas_call x1, Pallas kernels, local(): pl.pallas_call(functools.partial(kernel, n_seq, n_grp), out_shape=jax.Sha...  384 us

profile of v1, /device:TPU:0, one launch (start us, length us, event | category | flops | bytes accessed | tf_op | source)
XLA Modules:
  0.0 389.1 jit_solution(3016003904573803870)
XLA Ops:
  0.0 0.0 copy-start
  0.0 1.5 reduce-precision_convert_fusion.1
  1.5 1.2 pad_maximum_fusion.proj
  2.7 0.0 copy-done
  2.7 0.6 reshape.3.out_gain
  3.3 383.9 %shard_map.64 = bf16[512,512]{1,0:T(8,128)(2,1)} custom-call(bf16[512,512]{1,0:T(8,128)(2,1)} %hidden.1, bf16[3,256,1536]{2,1,0:T(8,128)(2,1)} %qkv_w.1, bf16[3,512,256]{2,1,0:T(8,128)(2,1)} %out_w.1, bf16[3,4,128,384]{3,2,1,0:T(8,128)(2,1)} %pad_maximum_fusion.proj, f32[3,2048]{1,0:T(4,128)} %norm_gain.1, f32[3,4,1,128]{3,2,1,0:T(1,128)} %reshape.3.out_gain), custom_call_target="tpu_custom_call" | custom-call | tf_op jit(solution)/shard_map/pallas_call | solution.py:297
  387.2 1.9 copy.8
Async XLA Ops:
  0.0 2.7 copy-start

commit v2 on v1

--- a/solution.py
+++ b/solution.py
@@ -18,6 +18,17 @@
     return pltpu.make_async_remote_copy(
         src_ref=src, dst_ref=dst, send_sem=send, recv_sem=recv, device_id=device, device_id_type=MESH
     )
+
+
+def exchange(line, step, lines):
+    if lines & (lines - 1):
+        return lax.rem(line + step, lines), lax.rem(line + lines - step, lines)
+    other, bit = line, 1
+    while bit < lines:
+        if step & bit:
+            other = other + bit * (1 - 2 * ((line // bit) % 2))
+        bit *= 2
+    return other, other
 
 
 def kernel(
@@ -40,6 +51,14 @@
     pair = line * 2 + 1 - parity
 
     stores = ((qkv_w, wq), (out_w, wo))
+    halves = 2
+    cut_rows = rows // halves
+
+    def piece(l, k, owner):
+        if k == halves:
+            return wo.at[l, owner]
+        return wq.at[l, owner, pl.ds(k * cut_rows, cut_rows)]
+
     own_copies = [
         [pltpu.make_async_copy(src.at[l], dst.at[l, me], local_sem.at[1 + 2 * l + k]) for k, (src, dst) in enumerate(stores)]
         for l in range(layers)
@@ -59,30 +78,38 @@
     pl.semaphore_wait(barrier, lines + n_grp - 1)
 
     def z_copy(l, k, step):
-        ref = stores[k][1].at[l, me]
-        to = lax.rem(line + step, lines) * 2 + parity
+        ref = piece(l, k, me)
+        to = exchange(line, step, lines)[0] * 2 + parity
         return remote(ref, ref, z_send.at[l, k, step], z_recv.at[l, k, line], {"seq": to})
 
     def z_arrival(l, k, step):
-        src = lax.rem(line + lines - step, lines)
-        ref = stores[k][1].at[l, src * 2 + parity]
+        src = exchange(line, step, lines)[1]
+        ref = piece(l, k, src * 2 + parity)
         return remote(ref, ref, z_send.at[l, k, step], z_recv.at[l, k, src], {"seq": src * 2 + parity})
 
     def y_copy(l, k, step):
-        src = lax.rem(line + lines - step, lines)
-        ref = stores[k][1].at[l, src * 2 + parity]
+        src = exchange(line, step, lines)[1]
+        ref = piece(l, k, src * 2 + parity)
         return remote(ref, ref, y_send.at[l, k, src], y_recv.at[l, k, src], {"seq": pair})
 
     def y_arrival(l, k, step):
-        src = lax.rem(line + lines - step, lines)
-        ref = stores[k][1].at[l, src * 2 + 1 - parity]
+        src = exchange(line, step, lines)[1]
+        ref = piece(l, k, src * 2 + 1 - parity)
         return remote(ref, ref, y_send.at[l, k, src], y_recv.at[l, k, src], {"seq": pair})
 
-    def send_weights(l, k):
-        own_copies[l][k].wait()
-        for step in range(1, lines):
-            z_copy(l, k, step).start()
-        y_copy(l, k, 0).start()
+    order = list(range(1, lines))
+    arrivals = [(k, step) for k in range(halves) for step in order]
+
+    def send_weights(l):
+        for c in own_copies[l]:
+            c.wait()
+        for k in range(halves + 1):
+            for step in order:
+                z_copy(l, k, step).start()
+
+    def pair_weights(l):
+        for k in range(halves + 1):
+            y_copy(l, k, 0).start()
 
     def forward(l, k, step):
         z_arrival(l, k, step).wait_recv()
@@ -120,8 +147,8 @@
     own_hidden.wait()
     for k in range(1, n_grp):
         ag_copy(0, k).start()
-    send_weights(0, 0)
-    send_weights(0, 1)
+    send_weights(0)
+    pair_weights(0)
 
     scale = head ** (-0.25)
     inv = 1.0 / math.sqrt(feats)
@@ -150,10 +177,11 @@
                 cut = slice(g * width, (g + 1) * width)
                 normed[at, cut] = (wide[g] * rms * norm_gain[l : l + 1, cut]).astype(bf16)
 
-        for step in range(1 + forwarded, lines):
-            forward(l, 0, step)
-        for step in range(lines):
-            y_arrival(l, 0, step).wait_recv()
+        for k, step in arrivals[forwarded:]:
+            forward(l, k, step)
+        for k in range(halves):
+            for step in range(lines):
+                y_arrival(l, k, step).wait_recv()
 
         @pl.loop(0, heads)
         def _(h):
@@ -174,8 +202,6 @@
             st_send[l, h, feats:] = z.astype(bf16)
 
         pair_copy(l).start()
-        for step in range(1, lines):
-            forward(l, 1, step)
         pair_copy(l).wait_recv()
 
         @pl.loop(0, heads)
@@ -188,8 +214,11 @@
                 line_copy(l, step).start()
 
         if not last:
-            send_weights(l + 1, 0)
-            send_weights(l + 1, 1)
+            send_weights(l + 1)
+        for step in order:
+            forward(l, halves, step)
+        if not last:
+            pair_weights(l + 1)
 
         @pl.loop(0, heads)
         def _(h):
@@ -227,7 +256,7 @@
             att[:, pl.ds(pl.multiple_of(h * head, 128), head)] = (a * norm * out_gain[l, h]).astype(bf16)
 
         for step in range(lines):
-            y_arrival(l, 1, step).wait_recv()
+            y_arrival(l, halves, step).wait_recv()
         per = width // oc
         for k in list(range(1, n_grp)) + [0]:
             to = lax.rem(grp + k, n_grp)
@@ -239,8 +268,9 @@
                 rs_copy(l, k).start()
         forwarded = 0
         if not last and lines > 1:
-            forward(l + 1, 0, 1)
-            forwarded = 1
+            forwarded = min(2, len(arrivals))
+            for k, step in arrivals[:forwarded]:
+                forward(l + 1, k, step)
         for k in range(1, n_grp):
             rs_copy(l, k).wait_send()
             rs_arrival(l, k).wait_recv()
@@ -260,13 +290,14 @@
         if not last:
             for k in range(1, n_grp):
                 ag_copy(l + 1, k).start()
-            if lines > 2:
-                forward(l + 1, 0, 2)
-                forwarded = 2
+            ready = min(4, len(arrivals))
+            for k, step in arrivals[forwarded:ready]:
+                forward(l + 1, k, step)
+            forwarded = ready
 
     for l in range(layers):
         pair_copy(l).wait_send()
-        for k in range(2):
+        for k in range(halves + 1):
             for step in range(1, lines):
                 z_copy(l, k, step).wait_send()
             for step in range(lines):
@@ -319,10 +350,10 @@
             pltpu.VMEM((layers, lines) + state, bf16),
             pltpu.VMEM(state, f32),
             dma((1 + 2 * layers,)),
-            dma((layers, 2, lines)),
-            dma((layers, 2, lines)),
-            dma((layers, 2, lines)),
-            dma((layers, 2, lines)),
+            dma((layers, 3, lines)),
+            dma((layers, 3, lines)),
+            dma((layers, 3, lines)),
+            dma((layers, 3, lines)),
             dma((layers,)),
             dma((layers,)),
             dma((layers, lines)),

time: 393 us -> 362 us (0.921)
  the two profiles are of different devices: /device:TPU:0 before, /device:TPU:23 now
where the time goes in v2:
time: 362 us
  Pallas kernels  357 us (99%)
    pallas_call x1, Pallas kernels, local(): pl.pallas_call(functools.partial(kernel, n_seq, n_grp), out_shape=jax.Sha...  357 us

profile of v2, /device:TPU:23, one launch (start us, length us, event | category | flops | bytes accessed | tf_op | source)
XLA Modules:
  0.0 362.2 jit_solution(1192471039272497922)
XLA Ops:
  0.0 0.0 copy-start
  0.0 1.5 reduce-precision_convert_fusion.1
  1.5 1.2 pad_maximum_fusion.proj
  2.7 0.0 copy-done
  2.7 0.6 reshape.3.out_gain
  3.3 357.1 %shard_map.64 = bf16[512,512]{1,0:T(8,128)(2,1)} custom-call(bf16[512,512]{1,0:T(8,128)(2,1)} %hidden.1, bf16[3,256,1536]{2,1,0:T(8,128)(2,1)} %qkv_w.1, bf16[3,512,256]{2,1,0:T(8,128)(2,1)} %out_w.1, bf16[3,4,128,384]{3,2,1,0:T(8,128)(2,1)} %pad_maximum_fusion.proj, f32[3,2048]{1,0:T(4,128)} %norm_gain.1, f32[3,4,1,128]{3,2,1,0:T(1,128)} %reshape.3.out_gain), custom_call_target="tpu_custom_call" | custom-call | tf_op jit(solution)/shard_map/pallas_call | solution.py:328
  360.4 1.9 copy.8
Async XLA Ops:
  0.0 2.7 copy-start
